TPU v7x, 32 devices: a whole 2x2x4 slice. The times are simulated.
32 devices in a mesh: pb: 4 (over x, core), ka: 8 (over z, y).
Axes of the slice: x: 2, y: 2, z: 4, core: 2. Of those that a mesh axis runs over, the one named last changes fastest.
Arguments:
- queries: bfloat16 [4096, 1024], P(('pb', 'ka')), may hold values from -6 to 6
- key_rows: bfloat16 [4096, 128], P(('pb', 'ka')), may hold values from -6 to 6
- value_rows: bfloat16 [4096, 128], P(('pb', 'ka')), may hold values from -6 to 6
- forward_out: bfloat16 [4096, 1024], P(('pb', 'ka')), may hold values from -6 to 6
- out_grad: bfloat16 [4096, 1024], P(('pb', 'ka')), may hold values from -4 to 4
- logsumexp: float32 [8, 4096], P(None, ('pb', 'ka')), may hold values from 3 to 7
- position: int32 [4096], P(('pb', 'ka')), may hold values from 0 to 4095, as said below
- segment: int32 [4096], P(('pb', 'ka')), may hold values from 0 to 7, as said below
Outputs:
- query_grad: bfloat16 [4096, 1024], P(('pb', 'ka'))
- key_grad: bfloat16 [4096, 128], P(('pb', 'ka'))
- value_grad: bfloat16 [4096, 128], P(('pb', 'ka'))
Inputs may be any that keep to these rules, and one draw needn't show every extreme that they name: `position`: a permutation of 0 to 4095; each aligned run of 128 rows holds 128 consecutive positions in increasing order. `segment`: the document of the row's position; each document is a nonempty run of consecutive positions, numbered in the order of positions, 8 documents in all.
All inputs are finite; a program needn't handle non-finite values.
Results may differ from a plain program's by a relative error of at most 0.0051.
Values may be sent and summed in bfloat16 or wider, within the bound.
A program may use at most 64 MiB of HBM per device.

v0:
```python
import functools

import jax
import jax.numpy as jnp
from jax import lax
from jax.experimental import pallas as pl
from jax.experimental.pallas import tpu as pltpu
from jax.sharding import PartitionSpec as P

MESH = pl.DeviceIdType.MESH
LOG2E = 1.4426950408889634
HIDDEN = -1e30
NT = (((1,), (1,)), ((), ()))
F32 = jnp.float32
BF16 = jnp.bfloat16


def kernel(
    pb_size, ka_size,
    q_hbm, g_hbm, o_hbm, k_hbm, v_hbm, lse_ref, place_ref, doc_ref,
    dq_ref, dk_ref, dv_ref,
    kv, qs, gs, os, own, sp, bias, pt, st, dqt, dqr,
    part, red, col, zpart, zred,
    load, kv_send, kv_recv, relay_send, relay_recv, pair_send, pair_recv,
    red_send, red_recv, z_send, z_recv,
):
    rows, width = dk_ref.shape
    heads = q_hbm.shape[1] // width
    both = 2 * rows
    scale = width ** (-0.5)
    nz, plane = ka_size // 2, pb_size
    pb, ka = lax.axis_index("pb"), lax.axis_index("ka")
    hi, core = pb // 2, lax.rem(pb, 2)
    z, low = ka // 2, lax.rem(ka, 2)

    def place(dz, dp):
        up, bit = z, 1
        while bit < nz:
            mine, flip = (z // bit) % 2, (dz // bit) % 2
            up = up + flip * (1 - 2 * mine) * bit
            bit *= 2
        far = 1 - hi if dp // 2 else hi
        near = 1 - low if dp % 2 else low
        return {"pb": far * 2 + core, "ka": up * 2 + near}

    partner = {"pb": hi * 2 + 1 - core, "ka": ka}

    def remote(src, dst, send, recv, device):
        return pltpu.make_async_remote_copy(
            src_ref=src, dst_ref=dst, send_sem=send, recv_sem=recv,
            device_id=device, device_id_type=MESH,
        )

    loads = [
        pltpu.make_async_copy(k_hbm, kv.at[0, 0, pl.ds(0, rows)], load.at[0]),
        pltpu.make_async_copy(v_hbm, kv.at[0, 0, pl.ds(rows, rows)], load.at[1]),
    ]
    for src, dst in ((q_hbm, qs), (g_hbm, gs), (o_hbm, os)):
        for h in range(heads):
            loads.append(pltpu.make_async_copy(
                src.at[:, pl.ds(h * width, width)], dst.at[h, pl.ds(0, rows)], load.at[len(loads)]
            ))
    for copy in loads:
        copy.start()

    barrier = pltpu.get_barrier_semaphore()
    peers = [place(dz, 0) for dz in range(1, nz)] + [place(0, dp) for dp in range(1, plane)] + [partner]
    for peer in peers:
        pl.semaphore_signal(barrier, inc=1, device_id=peer, device_id_type=MESH)

    spots = place_ref[...].astype(F32)
    docs = doc_ref[...].astype(F32)
    line = lax.broadcasted_iota(jnp.int32, (16, rows), 0)
    first = jnp.min(spots, axis=1, keepdims=True) * (1.0 / rows)
    meta = jnp.where(line == 0, jnp.broadcast_to(first, (16, rows)), jnp.broadcast_to(docs, (16, rows)))
    kv[0, 0, both:both + 16, :] = meta.astype(BF16)
    own[:heads] = lse_ref[...]
    own[2 * heads:2 * heads + 8] = jnp.where(
        line[:8] == 0, jnp.broadcast_to(spots, (8, rows)), jnp.broadcast_to(docs, (8, rows))
    )
    for copy in loads[:2]:
        copy.wait()
    pl.semaphore_wait(barrier, len(peers))

    def column_copy(dz):
        return remote(kv.at[0, 0], kv.at[dz, 0], kv_send.at[dz, 0], kv_recv.at[dz, 0], place(dz, 0))

    def plane_copy(dz, dp):
        return remote(kv.at[dz, 0], kv.at[dz, dp], kv_send.at[dz, dp], kv_recv.at[dz, dp], place(0, dp))

    def relay_copy(dz, dp):
        piece = pl.ds(0, rows) if dp == 1 else pl.ds(rows, rows + 16)
        return remote(
            kv.at[dz, 3 - dp, piece], kv.at[dz, 3, piece],
            relay_send.at[dz, dp - 1], relay_recv.at[dz, dp - 1], place(0, dp),
        )

    def part_copy(dz, dp):
        return remote(part.at[dz, dp], red.at[dz, dp], red_send.at[dz, dp], red_recv.at[dz, dp], place(0, dp))

    def z_copy(dz):
        return remote(zpart.at[dz], zred.at[dz], z_send.at[dz], z_recv.at[dz], place(dz, 0))

    ours, theirs = pl.ds(0, rows), pl.ds(rows, rows)
    pair = [
        remote(src, dst, pair_send.at[i], pair_recv.at[i], partner)
        for i, (src, dst) in enumerate((
            (qs.at[:, ours], qs.at[:, theirs]), (gs.at[:, ours], gs.at[:, theirs]),
            (own, sp), (dqt.at[1], dqr),
        ))
    ]
    for dp in (1, 2):
        plane_copy(0, dp).start()
    for dz in range(1, nz):
        column_copy(dz).start()
    dqt[...] = jnp.zeros_like(dqt)
    for copy in loads[2:2 + 2 * heads]:
        copy.wait()
    for copy in pair[:2]:
        copy.start()
    for copy in loads[2 + 2 * heads:]:
        copy.wait()
    for h in range(heads):
        product = gs[h, :rows].astype(F32) * os[h].astype(F32)
        own[heads + h:heads + h + 1] = jnp.sum(product.T, axis=0, keepdims=True)
    pair[2].start()

    def spread(dz):
        column_copy(dz).wait_recv()
        for dp in (1, 2):
            plane_copy(dz, dp).start()

    def pass_on(dz):
        for dp in (2, 1):
            plane_copy(dz, 3 - dp).wait_recv()
            relay_copy(dz, dp).start()

    pass_on(0)
    spread(1)
    if nz > 2:
        spread(2)
    pass_on(1)
    for copy in pair[:3]:
        copy.wait_recv()

    def stat_row(i):
        return jnp.concatenate([own[i:i + 1, :], sp[i:i + 1, :]], axis=1)

    place_q = stat_row(2 * heads)
    doc_q = stat_row(2 * heads + 1)

    def key_side(dz, dp):
        meta = kv[dz, dp, both:both + 16, :].astype(F32)
        base = jnp.broadcast_to(meta[0:1, :], (rows, rows))
        doc = jnp.broadcast_to(meta[1:2, :], (rows, rows)).T
        spot = base * float(rows) + lax.broadcasted_iota(jnp.int32, (rows, rows), 0).astype(F32)
        return spot, doc

    def step(dz, dp):
        for i in range(2):
            spot, doc = key_side(dz, dp + i)
            for c in range(2):
                lanes = slice(c * rows, (c + 1) * rows)
                seen = (spot <= place_q[:, lanes]) & (doc == doc_q[:, lanes])
                bias[i * rows:(i + 1) * rows, lanes] = jnp.where(seen, 0.0, HIDDEN)
        kb = jnp.concatenate([kv[dz, dp, :rows, :], kv[dz, dp + 1, :rows, :]], axis=0)
        vb = jnp.concatenate([kv[dz, dp, rows:both, :], kv[dz, dp + 1, rows:both, :]], axis=0)
        kt = kb.T
        for h in range(heads):
            s = lax.dot_general(kb, qs[h], NT, preferred_element_type=F32)
            d = lax.dot_general(vb, gs[h], NT, preferred_element_type=F32)
            w = jnp.exp2(s * (scale * LOG2E) + (bias[...] - stat_row(h) * LOG2E))
            pt[:, h * both:(h + 1) * both] = w.astype(BF16)
            st[:, h * both:(h + 1) * both] = (w * (d - stat_row(heads + h))).astype(BF16)
        dv = jnp.dot(pt[...], gs[...].reshape(heads * both, width), preferred_element_type=F32)
        dk = jnp.dot(st[...], qs[...].reshape(heads * both, width), preferred_element_type=F32)
        for i in range(2):
            piece = slice(i * rows, (i + 1) * rows)
            if dp + i == 0:
                col[dz, :rows] = dk[piece]
                col[dz, rows:] = dv[piece]
            else:
                part[dz, dp + i, :rows] = dk[piece].astype(BF16)
                part[dz, dp + i, rows:] = dv[piece].astype(BF16)
                part_copy(dz, dp + i).start()
        for h in range(heads):
            dq = jnp.dot(kt, st[:, h * both:(h + 1) * both], preferred_element_type=F32)
            dqt[0, h] += dq[:, :rows]
            dqt[1, h] += dq[:, rows:]

    def plane_sum(dz):
        total = col[dz]
        for dp in range(1, plane):
            part_copy(dz, dp).wait_recv()
            total = total + red[dz, dp].astype(F32)
        return total

    def send_sum(dz):
        zpart[dz] = plane_sum(dz).astype(BF16)
        z_copy(dz).start()

    def group(turn, carry):
        dz = lax.rem(turn + 1, nz)

        @pl.when(turn + 3 < nz)
        def _():
            spread(turn + 3)

        step(dz, 0)

        @pl.when(turn + 2 < nz)
        def _():
            pass_on(turn + 2)

        for dp in (1, 2):
            relay_copy(dz, dp).wait_recv()
        step(dz, 2)

        @pl.when(turn > 0)
        def _():
            send_sum(turn)

        return carry

    lax.fori_loop(0, nz, group, 0)
    pair[3].start()
    pair[3].wait_recv()
    for h in range(heads):
        dq = (dqt[0, h] + dqr[h]) * scale
        dq_ref[:, h * width:(h + 1) * width] = dq.T.astype(BF16)
    total = plane_sum(0)
    for dz in range(1, nz):
        z_copy(dz).wait_recv()
        total = total + zred[dz].astype(F32)
    dk_ref[...] = (total[:rows] * scale).astype(BF16)
    dv_ref[...] = total[rows:].astype(BF16)

    for copy in pair:
        copy.wait_send()
    for dz in range(nz):
        for dp in range(1, plane):
            part_copy(dz, dp).wait_send()
        for dp in (1, 2):
            plane_copy(dz, dp).wait_send()
            relay_copy(dz, dp).wait_send()
        if dz > 0:
            column_copy(dz).wait_send()
            z_copy(dz).wait_send()


def write_out(*refs):
    for src, dst in zip(refs[:3], refs[3:]):
        dst[...] = src[...]


def solution(mesh):
    pb_size, ka_size = mesh.shape["pb"], mesh.shape["ka"]

    def body(queries, key_rows, value_rows, forward_out, out_grad, logsumexp, position, segment):
        rows, width = key_rows.shape
        heads = queries.shape[1] // width
        nz, plane = ka_size // 2, pb_size
        both = 2 * rows
        dma, vmem = pltpu.SemaphoreType.DMA, pltpu.VMEM
        space = pl.BlockSpec(memory_space=pltpu.VMEM)
        grads = pl.pallas_call(
            functools.partial(kernel, pb_size, ka_size),
            out_shape=(
                jax.ShapeDtypeStruct(queries.shape, BF16),
                jax.ShapeDtypeStruct(key_rows.shape, BF16),
                jax.ShapeDtypeStruct(key_rows.shape, BF16),
            ),
            in_specs=[pl.BlockSpec(memory_space=pl.ANY)] * 5 + [space] * 3,
            out_specs=(space,) * 3,
            scratch_shapes=[
                vmem((nz, plane, both + 16, width), BF16),
                vmem((heads, both, width), BF16),
                vmem((heads, both, width), BF16),
                vmem((heads, rows, width), BF16),
                vmem((2 * heads + 8, rows), F32),
                vmem((2 * heads + 8, rows), F32),
                vmem((both, both), F32),
                vmem((both, heads * both), BF16),
                vmem((both, heads * both), BF16),
                vmem((2, heads, width, rows), F32),
                vmem((heads, width, rows), F32),
                vmem((nz, plane, both, width), BF16),
                vmem((nz, plane, both, width), BF16),
                vmem((nz, both, width), F32),
                vmem((nz, both, width), BF16),
                vmem((nz, both, width), BF16),
                dma((3 * heads + 2,)), dma((nz, plane)), dma((nz, plane)),
                dma((nz, 2)), dma((nz, 2)), dma((4,)), dma((4,)),
                dma((nz, plane)), dma((nz, plane)),
                dma((nz,)), dma((nz,)),
            ],
            compiler_params=pltpu.CompilerParams(
                collective_id=0, has_side_effects=True, vmem_limit_bytes=56 * 2**20
            ),
        )(
            queries, out_grad, forward_out, key_rows, value_rows, logsumexp,
            position.reshape(1, rows), segment.reshape(1, rows),
        )
        return pl.pallas_call(
            write_out,
            out_shape=tuple(jax.ShapeDtypeStruct(g.shape, g.dtype) for g in grads),
            in_specs=[space] * 3,
            out_specs=(space,) * 3,
        )(*grads)

    flat = P(("pb", "ka"), None)
    line = P(("pb", "ka"))
    return jax.shard_map(
        body,
        mesh=mesh,
        in_specs=(flat,) * 5 + (P(None, ("pb", "ka")), line, line),
        out_specs=(flat,) * 3,
        check_vma=False,
    )
```

profile of v0, /device:TPU:0, one launch (start us, length us, event | category | flops | bytes accessed | tf_op | source)
XLA Modules:
  0.0 40.4 jit_solution(4784714645909422234)
XLA Ops:
  0.6 38.0 %shard_map.103 = (bf16[128,1024]{1,0:T(8,128)(2,1)}, bf16[128,128]{1,0:T(8,128)(2,1)}, bf16[128,128]{1,0:T(8,128)(2,1)}) custom-call(bf16[128,1024]{1,0:T(8,128)(2,1)} %q_hbm.1, bf16[128,1024]{1,0:T(8,128)(2,1)} %g_hbm.1, bf16[128,1024]{1,0:T(8,128)(2,1)} %o_hbm.1, bf16[128,128]{1,0:T(8,128)(2,1)} %k_hbm.1, bf16[128,128]{1,0:T(8,128)(2,1)} %v_hbm.1, ...), custom_call_target="tpu_custom_call" | custom-call | tf_op jit(solution)/shard_map/pallas_call | solution.py:266
  38.7 1.7 %shard_map.104 = (bf16[128,1024]{1,0:T(8,128)(2,1)}, bf16[128,128]{1,0:T(8,128)(2,1)}, bf16[128,128]{1,0:T(8,128)(2,1)}) custom-call(bf16[128,1024]{1,0:T(8,128)(2,1)} %get-tuple-element.6.refs_0_, bf16[128,128]{1,0:T(8,128)(2,1)} %get-tuple-element.7.refs_1_, bf16[128,128]{1,0:T(8,128)(2,1)} %get-tuple-element.8.refs_2_), custom_call_target="tpu_custom_call" | custom-call | tf_op jit(solution)/shard_map/pallas_call | solution.py:304
where the time goes:
time: 40.6 us; the launch traced here: 40.4 us
  Pallas kernels  39.7 us (98%)
  between operations  0.64 us (2%)
    pallas_call x1, Pallas kernels, body(): pl.pallas_call(functools.partial(kernel, pb_size, ka_size), out_shape=(ja...  38 us
    pallas_call x1, Pallas kernels, body(): pl.pallas_call(write_out, out_shape=tuple((jax.ShapeDtypeStruct(g.shape,...  1.7 us

commit v1 on v0

--- a/solution.py
+++ b/solution.py
@@ -15,14 +15,24 @@
 BF16 = jnp.bfloat16
 
 
+def schedule(nz):
+    late = (0.0, 1.3, 1.4, 2.6)
+    order = sorted((dz + late[dp], dz, dp) for dz in range(nz) for dp in range(4))
+    blocks = [b[1:] for b in order]
+    steps = [blocks[i:i + 2] for i in range(0, len(blocks), 2)]
+    when = {b: t for t, step in enumerate(steps) for b in step}
+    folded = list(range(1, nz // 2))
+    return steps, when, list(range(nz // 2, nz)), folded
+
+
 def kernel(
     pb_size, ka_size,
     q_hbm, g_hbm, o_hbm, k_hbm, v_hbm, lse_ref, place_ref, doc_ref,
     dq_ref, dk_ref, dv_ref,
     kv, qs, gs, os, own, sp, bias, pt, st, dqt, dqr,
-    part, red, col, zpart, zred,
+    part, red, acc, zpart, zred, fold,
     load, kv_send, kv_recv, relay_send, relay_recv, pair_send, pair_recv,
-    red_send, red_recv, z_send, z_recv,
+    red_send, red_recv, z_send, z_recv, fold_send, fold_recv,
 ):
     rows, width = dk_ref.shape
     heads = q_hbm.shape[1] // width
@@ -64,7 +74,10 @@
         copy.start()
 
     barrier = pltpu.get_barrier_semaphore()
+    steps, when, direct, folded = schedule(nz)
+    last = len(steps) - 1
     peers = [place(dz, 0) for dz in range(1, nz)] + [place(0, dp) for dp in range(1, plane)] + [partner]
+    peers += [place(dz, 3) for dz in direct]
     for peer in peers:
         pl.semaphore_signal(barrier, inc=1, device_id=peer, device_id_type=MESH)
 
@@ -96,7 +109,11 @@
         )
 
     def part_copy(dz, dp):
-        return remote(part.at[dz, dp], red.at[dz, dp], red_send.at[dz, dp], red_recv.at[dz, dp], place(0, dp))
+        far = dz if dp == 3 and dz in direct else 0
+        return remote(part.at[dz, dp], red.at[dz, dp], red_send.at[dz, dp], red_recv.at[dz, dp], place(far, dp))
+
+    def fold_copy(dz):
+        return remote(part.at[dz, 3], fold.at[dz], fold_send.at[dz], fold_recv.at[dz], place(dz, 0))
 
     def z_copy(dz):
         return remote(zpart.at[dz], zred.at[dz], z_send.at[dz], z_recv.at[dz], place(dz, 0))
@@ -113,6 +130,7 @@
         plane_copy(0, dp).start()
     for dz in range(1, nz):
         column_copy(dz).start()
+    plane_copy(0, 3).start()
     dqt[...] = jnp.zeros_like(dqt)
     for copy in loads[2:2 + 2 * heads]:
         copy.wait()
@@ -135,11 +153,6 @@
             plane_copy(dz, 3 - dp).wait_recv()
             relay_copy(dz, dp).start()
 
-    pass_on(0)
-    spread(1)
-    if nz > 2:
-        spread(2)
-    pass_on(1)
     for copy in pair[:3]:
         copy.wait_recv()
 
@@ -156,15 +169,16 @@
         spot = base * float(rows) + lax.broadcasted_iota(jnp.int32, (rows, rows), 0).astype(F32)
         return spot, doc
 
-    def step(dz, dp):
-        for i in range(2):
-            spot, doc = key_side(dz, dp + i)
+    def step(blocks):
+        (za, pa), (zb, pc) = blocks
+        for i, (dz, dp) in enumerate(blocks):
+            spot, doc = key_side(dz, dp)
             for c in range(2):
                 lanes = slice(c * rows, (c + 1) * rows)
                 seen = (spot <= place_q[:, lanes]) & (doc == doc_q[:, lanes])
                 bias[i * rows:(i + 1) * rows, lanes] = jnp.where(seen, 0.0, HIDDEN)
-        kb = jnp.concatenate([kv[dz, dp, :rows, :], kv[dz, dp + 1, :rows, :]], axis=0)
-        vb = jnp.concatenate([kv[dz, dp, rows:both, :], kv[dz, dp + 1, rows:both, :]], axis=0)
+        kb = jnp.concatenate([kv[za, pa, :rows, :], kv[zb, pc, :rows, :]], axis=0)
+        vb = jnp.concatenate([kv[za, pa, rows:both, :], kv[zb, pc, rows:both, :]], axis=0)
         kt = kb.T
         for h in range(heads):
             s = lax.dot_general(kb, qs[h], NT, preferred_element_type=F32)
@@ -174,23 +188,20 @@
             st[:, h * both:(h + 1) * both] = (w * (d - stat_row(heads + h))).astype(BF16)
         dv = jnp.dot(pt[...], gs[...].reshape(heads * both, width), preferred_element_type=F32)
         dk = jnp.dot(st[...], qs[...].reshape(heads * both, width), preferred_element_type=F32)
-        for i in range(2):
+        for i, (dz, dp) in enumerate(blocks):
             piece = slice(i * rows, (i + 1) * rows)
-            if dp + i == 0:
-                col[dz, :rows] = dk[piece]
-                col[dz, rows:] = dv[piece]
-            else:
-                part[dz, dp + i, :rows] = dk[piece].astype(BF16)
-                part[dz, dp + i, rows:] = dv[piece].astype(BF16)
-                part_copy(dz, dp + i).start()
+            acc[dz, dp, :rows] = dk[piece]
+            acc[dz, dp, rows:] = dv[piece]
+            part[dz, dp, :rows] = dk[piece].astype(BF16)
+            part[dz, dp, rows:] = dv[piece].astype(BF16)
         for h in range(heads):
             dq = jnp.dot(kt, st[:, h * both:(h + 1) * both], preferred_element_type=F32)
             dqt[0, h] += dq[:, :rows]
             dqt[1, h] += dq[:, rows:]
 
     def plane_sum(dz):
-        total = col[dz]
-        for dp in range(1, plane):
+        total = acc[dz, 0]
+        for dp in (1, 2):
             part_copy(dz, dp).wait_recv()
             total = total + red[dz, dp].astype(F32)
         return total
@@ -199,36 +210,69 @@
         zpart[dz] = plane_sum(dz).astype(BF16)
         z_copy(dz).start()
 
-    def group(turn, carry):
-        dz = lax.rem(turn + 1, nz)
-
-        @pl.when(turn + 3 < nz)
-        def _():
-            spread(turn + 3)
-
-        step(dz, 0)
-
-        @pl.when(turn + 2 < nz)
-        def _():
-            pass_on(turn + 2)
-
-        for dp in (1, 2):
-            relay_copy(dz, dp).wait_recv()
-        step(dz, 2)
-
-        @pl.when(turn > 0)
-        def _():
-            send_sum(turn)
-
+    def corner():
+        total = acc[0, 3]
+        for dz in folded:
+            fold_copy(dz).wait_recv()
+            total = total + fold[dz].astype(F32)
+        part[0, 3] = total.astype(BF16)
+        part_copy(0, 3).start()
+
+    def before(t):
+        for dz in range(1, nz):
+            if max(0, when[dz, 0] - 1) == t:
+                spread(dz)
+        for b in steps[t]:
+            if b[0] == 0 and b[1] > 0:
+                plane_copy(*b).wait_recv()
+        for dz in range(1, nz):
+            if min(when[dz, 1], when[dz, 2]) == t:
+                pass_on(dz)
+        for b in steps[t]:
+            if b[0] > 0 and b[1] == 3:
+                for dp in (1, 2):
+                    relay_copy(b[0], dp).wait_recv()
+
+    def after(t):
+        for dz, dp in steps[t]:
+            if dp == 3 and dz in folded:
+                fold_copy(dz).start()
+            elif dp and (dz or dp < 3):
+                part_copy(dz, dp).start()
+        for dz in range(1, nz):
+            if max(when[dz, 0], when[dz, 1], when[dz, 2]) + 2 == t:
+                send_sum(dz)
+
+    def pick(t, table):
+        value = jnp.int32(table[-1])
+        for k in range(len(table) - 1):
+            value = jnp.where(t == k, table[k], value)
+        return value
+
+    def turn(t, carry):
+        for k in range(len(steps)):
+            pl.when(t == k)(functools.partial(before, k))
+        step([[pick(t, [s[i][j] for s in steps]) for j in range(2)] for i in range(2)])
+        for k in range(len(steps)):
+            pl.when(t == k)(functools.partial(after, k))
         return carry
 
-    lax.fori_loop(0, nz, group, 0)
+    lax.fori_loop(0, len(steps), turn, 0)
     pair[3].start()
+    for dz in range(1, nz):
+        if max(when[dz, 0], when[dz, 1], when[dz, 2]) + 2 > last:
+            send_sum(dz)
+    corner()
     pair[3].wait_recv()
     for h in range(heads):
         dq = (dqt[0, h] + dqr[h]) * scale
         dq_ref[:, h * width:(h + 1) * width] = dq.T.astype(BF16)
     total = plane_sum(0)
+    part_copy(0, 3).wait_recv()
+    total = total + red[0, 3].astype(F32)
+    for dz in direct:
+        part_copy(dz, 3).wait_recv()
+        total = total + red[dz, 3].astype(F32)
     for dz in range(1, nz):
         z_copy(dz).wait_recv()
         total = total + zred[dz].astype(F32)
@@ -238,14 +282,19 @@
     for copy in pair:
         copy.wait_send()
     for dz in range(nz):
-        for dp in range(1, plane):
+        for dp in (1, 2):
             part_copy(dz, dp).wait_send()
-        for dp in (1, 2):
             plane_copy(dz, dp).wait_send()
-            relay_copy(dz, dp).wait_send()
+            if dz > 0:
+                relay_copy(dz, dp).wait_send()
+        if dz in folded:
+            fold_copy(dz).wait_send()
+        else:
+            part_copy(dz, 3).wait_send()
         if dz > 0:
             column_copy(dz).wait_send()
             z_copy(dz).wait_send()
+    plane_copy(0, 3).wait_send()
 
 
 def write_out(*refs):
@@ -270,7 +319,7 @@
                 jax.ShapeDtypeStruct(key_rows.shape, BF16),
                 jax.ShapeDtypeStruct(key_rows.shape, BF16),
             ),
-            in_specs=[pl.BlockSpec(memory_space=pl.ANY)] * 5 + [space] * 3,
+            in_specs=[pl.BlockSpec(memory_space=pltpu.HBM)] * 5 + [space] * 3,
             out_specs=(space,) * 3,
             scratch_shapes=[
                 vmem((nz, plane, both + 16, width), BF16),
@@ -286,26 +335,28 @@
                 vmem((heads, width, rows), F32),
                 vmem((nz, plane, both, width), BF16),
                 vmem((nz, plane, both, width), BF16),
-                vmem((nz, both, width), F32),
+                vmem((nz, plane, both, width), F32),
+                vmem((nz, both, width), BF16),
                 vmem((nz, both, width), BF16),
                 vmem((nz, both, width), BF16),
                 dma((3 * heads + 2,)), dma((nz, plane)), dma((nz, plane)),
                 dma((nz, 2)), dma((nz, 2)), dma((4,)), dma((4,)),
                 dma((nz, plane)), dma((nz, plane)),
-                dma((nz,)), dma((nz,)),
+                dma((nz,)), dma((nz,)), dma((nz,)), dma((nz,)),
             ],
             compiler_params=pltpu.CompilerParams(
-                collective_id=0, has_side_effects=True, vmem_limit_bytes=56 * 2**20
+                collective_id=0, has_side_effects=True, vmem_limit_bytes=48 * 2**20
             ),
-        )(
+        )(*(pltpu.with_memory_space_constraint(x, pltpu.HBM) for x in (
             queries, out_grad, forward_out, key_rows, value_rows, logsumexp,
             position.reshape(1, rows), segment.reshape(1, rows),
-        )
+        )))
         return pl.pallas_call(
             write_out,
             out_shape=tuple(jax.ShapeDtypeStruct(g.shape, g.dtype) for g in grads),
             in_specs=[space] * 3,
             out_specs=(space,) * 3,
+            compiler_params=pltpu.CompilerParams(vmem_limit_bytes=4 * 2**20),
         )(*grads)
 
     flat = P(("pb", "ka"), None)

time: 40.6 us -> 38.8 us (0.956)
  Pallas kernels: 39.7 us -> 37.9 us
    pallas_call x1, Pallas kernels: 1.7 us -> 0.74 us  [body(): pl.pallas_call(write_out, out_shape=tuple((jax.ShapeDtypeStruct(g.shape,...]
    pallas_call x1, Pallas kernels: 38 us -> 37.2 us  [body(): pl.pallas_call(functools.partial(kernel, pb_size, ka_size), out_shape=(ja...]
where the time goes in v1:
time: 38.8 us; the launch traced here: 38.6 us
  Pallas kernels  37.9 us (98%)
  between operations  0.64 us (2%)
    pallas_call x1, Pallas kernels, body(): pl.pallas_call(functools.partial(kernel, pb_size, ka_size), out_shape=(ja...  37.2 us

profile of v1, /device:TPU:0, one launch (start us, length us, event | category | flops | bytes accessed | tf_op | source)
XLA Modules:
  0.0 38.6 jit_solution(8872259748988180318)
XLA Ops:
  0.6 37.2 %shard_map.103 = (bf16[128,1024]{1,0:T(8,128)(2,1)S(1)}, bf16[128,128]{1,0:T(8,128)(2,1)S(1)}, bf16[128,128]{1,0:T(8,128)(2,1)S(1)}) custom-call(bf16[128,1024]{1,0:T(8,128)(2,1)} %q_hbm.1, bf16[128,1024]{1,0:T(8,128)(2,1)} %g_hbm.1, bf16[128,1024]{1,0:T(8,128)(2,1)} %o_hbm.1, bf16[128,128]{1,0:T(8,128)(2,1)} %k_hbm.1, bf16[128,128]{1,0:T(8,128)(2,1)} %v_hbm.1, ...), custom_call_target="tpu_custom_call" | custom-call | tf_op jit(solution)/shard_map/pallas_call | solution.py:315
  37.8 0.7 %shard_map.104 = (bf16[128,1024]{1,0:T(8,128)(2,1)}, bf16[128,128]{1,0:T(8,128)(2,1)}, bf16[128,128]{1,0:T(8,128)(2,1)}) custom-call(bf16[128,1024]{1,0:T(8,128)(2,1)S(1)} %get-tuple-element.6.refs_0_, bf16[128,128]{1,0:T(8,128)(2,1)S(1)} %get-tuple-element.7.refs_1_, bf16[128,128]{1,0:T(8,128)(2,1)S(1)} %get-tuple-element.8.refs_2_), custom_call_target="tpu_custom_call" | custom-call | tf_op jit(solution)/shard_map/pallas_call | solution.py:354

commit v2 on v1

--- a/solution.py
+++ b/solution.py
@@ -16,13 +16,20 @@
 
 
 def schedule(nz):
-    late = (0.0, 1.3, 1.4, 2.6)
-    order = sorted((dz + late[dp], dz, dp) for dz in range(nz) for dp in range(4))
+    ranks = [0, nz - 1] + list(range(1, nz - 1))
+    order = []
+    for r, dz in enumerate(ranks):
+        late = (0.0, 0.5, 0.6, 1.1) if r == 0 else (0.0, 1.3, 1.4, {1: 2.65, 2: 1.45}.get(r, 1.5))
+        order += [(r + late[dp], dz, dp) for dp in range(4)]
+    order.sort()
     blocks = [b[1:] for b in order]
     steps = [blocks[i:i + 2] for i in range(0, len(blocks), 2)]
     when = {b: t for t, step in enumerate(steps) for b in step}
-    folded = list(range(1, nz // 2))
-    return steps, when, list(range(nz // 2, nz)), folded
+    part = max(1, nz // 4)
+    climb = list(range(1, nz - 1))
+    direct = ranks[-part:]
+    folded = [dz for dz in range(1, part + 1) if dz not in direct]
+    return steps, when, climb, direct, folded, ranks
 
 
 def kernel(
@@ -74,10 +81,9 @@
         copy.start()
 
     barrier = pltpu.get_barrier_semaphore()
-    steps, when, direct, folded = schedule(nz)
+    steps, when, climb, direct, folded, ranks = schedule(nz)
     last = len(steps) - 1
     peers = [place(dz, 0) for dz in range(1, nz)] + [place(0, dp) for dp in range(1, plane)] + [partner]
-    peers += [place(dz, 3) for dz in direct]
     for peer in peers:
         pl.semaphore_signal(barrier, inc=1, device_id=peer, device_id_type=MESH)
 
@@ -108,12 +114,15 @@
             relay_send.at[dz, dp - 1], relay_recv.at[dz, dp - 1], place(0, dp),
         )
 
+    def climb_copy(dz):
+        return remote(kv.at[0, 3], kv.at[dz, 3], kv_send.at[dz, 3], kv_recv.at[dz, 3], place(dz, 0))
+
     def part_copy(dz, dp):
         far = dz if dp == 3 and dz in direct else 0
         return remote(part.at[dz, dp], red.at[dz, dp], red_send.at[dz, dp], red_recv.at[dz, dp], place(far, dp))
 
-    def fold_copy(dz):
-        return remote(part.at[dz, 3], fold.at[dz], fold_send.at[dz], fold_recv.at[dz], place(dz, 0))
+    def fold_copy(dz, dp):
+        return remote(part.at[dz, dp], fold.at[dz, dp], fold_send.at[dz, dp], fold_recv.at[dz, dp], place(dz, 0))
 
     def z_copy(dz):
         return remote(zpart.at[dz], zred.at[dz], z_send.at[dz], z_recv.at[dz], place(dz, 0))
@@ -128,7 +137,7 @@
     ]
     for dp in (1, 2):
         plane_copy(0, dp).start()
-    for dz in range(1, nz):
+    for dz in ranks[1:]:
         column_copy(dz).start()
     plane_copy(0, 3).start()
     dqt[...] = jnp.zeros_like(dqt)
@@ -151,7 +160,8 @@
     def pass_on(dz):
         for dp in (2, 1):
             plane_copy(dz, 3 - dp).wait_recv()
-            relay_copy(dz, dp).start()
+            if dz not in climb:
+                relay_copy(dz, dp).start()
 
     for copy in pair[:3]:
         copy.wait_recv()
@@ -201,7 +211,7 @@
 
     def plane_sum(dz):
         total = acc[dz, 0]
-        for dp in (1, 2):
+        for dp in () if dz in folded else (1, 2) if dz == 0 or dz in direct else (1, 2, 3):
             part_copy(dz, dp).wait_recv()
             total = total + red[dz, dp].astype(F32)
         return total
@@ -210,37 +220,47 @@
         zpart[dz] = plane_sum(dz).astype(BF16)
         z_copy(dz).start()
 
-    def corner():
-        total = acc[0, 3]
+    def merge(dp):
+        total = acc[0, dp]
         for dz in folded:
-            fold_copy(dz).wait_recv()
-            total = total + fold[dz].astype(F32)
-        part[0, 3] = total.astype(BF16)
-        part_copy(0, 3).start()
+            fold_copy(dz, dp).wait_recv()
+            total = total + fold[dz, dp].astype(F32)
+        part[0, dp] = total.astype(BF16)
+        part_copy(0, dp).start()
 
     def before(t):
-        for dz in range(1, nz):
-            if max(0, when[dz, 0] - 1) == t:
+        if t == when[0, 3]:
+            plane_copy(0, 3).wait_recv()
+            for dz in climb:
+                climb_copy(dz).start()
+        for r, dz in enumerate(ranks):
+            if r and max(0, when[dz, 0] - {1: 0, 2: 0}.get(r, 1)) == t:
                 spread(dz)
         for b in steps[t]:
-            if b[0] == 0 and b[1] > 0:
+            if b[0] == 0 and b[1] in (1, 2):
                 plane_copy(*b).wait_recv()
-        for dz in range(1, nz):
+        for dz in ranks[1:]:
             if min(when[dz, 1], when[dz, 2]) == t:
                 pass_on(dz)
         for b in steps[t]:
-            if b[0] > 0 and b[1] == 3:
+            if b[0] in climb and b[1] == 3:
+                climb_copy(b[0]).wait_recv()
+            elif b[0] > 0 and b[1] == 3:
                 for dp in (1, 2):
                     relay_copy(b[0], dp).wait_recv()
 
     def after(t):
         for dz, dp in steps[t]:
-            if dp == 3 and dz in folded:
-                fold_copy(dz).start()
-            elif dp and (dz or dp < 3):
+            if dp and dz in folded:
+                fold_copy(dz, dp).start()
+            elif dp and dz:
                 part_copy(dz, dp).start()
-        for dz in range(1, nz):
-            if max(when[dz, 0], when[dz, 1], when[dz, 2]) + 2 == t:
+        if t == last:
+            for dp in (3, 1, 2):
+                merge(dp)
+        for dz in ranks[1:]:
+            ready = when[dz, 0] if dz in folded else max(when[dz, dp] for dp in range(3 if dz in direct else 4)) + 2
+            if min(ready, last) == t:
                 send_sum(dz)
 
     def pick(t, table):
@@ -259,10 +279,6 @@
 
     lax.fori_loop(0, len(steps), turn, 0)
     pair[3].start()
-    for dz in range(1, nz):
-        if max(when[dz, 0], when[dz, 1], when[dz, 2]) + 2 > last:
-            send_sum(dz)
-    corner()
     pair[3].wait_recv()
     for h in range(heads):
         dq = (dqt[0, h] + dqr[h]) * scale
@@ -282,19 +298,21 @@
     for copy in pair:
         copy.wait_send()
     for dz in range(nz):
+        for dp in (1, 2, 3):
+            if dz in folded:
+                fold_copy(dz, dp).wait_send()
+            else:
+                part_copy(dz, dp).wait_send()
         for dp in (1, 2):
-            part_copy(dz, dp).wait_send()
             plane_copy(dz, dp).wait_send()
-            if dz > 0:
+            if dz > 0 and dz not in climb:
                 relay_copy(dz, dp).wait_send()
-        if dz in folded:
-            fold_copy(dz).wait_send()
-        else:
-            part_copy(dz, 3).wait_send()
         if dz > 0:
             column_copy(dz).wait_send()
             z_copy(dz).wait_send()
     plane_copy(0, 3).wait_send()
+    for dz in climb:
+        climb_copy(dz).wait_send()
 
 
 def write_out(*refs):
@@ -338,11 +356,11 @@
                 vmem((nz, plane, both, width), F32),
                 vmem((nz, both, width), BF16),
                 vmem((nz, both, width), BF16),
-                vmem((nz, both, width), BF16),
+                vmem((nz, plane, both, width), BF16),
                 dma((3 * heads + 2,)), dma((nz, plane)), dma((nz, plane)),
                 dma((nz, 2)), dma((nz, 2)), dma((4,)), dma((4,)),
                 dma((nz, plane)), dma((nz, plane)),
-                dma((nz,)), dma((nz,)), dma((nz,)), dma((nz,)),
+                dma((nz,)), dma((nz,)), dma((nz, plane)), dma((nz, plane)),
             ],
             compiler_params=pltpu.CompilerParams(
                 collective_id=0, has_side_effects=True, vmem_limit_bytes=48 * 2**20

time: 38.8 us -> 35.2 us (0.907)
  Pallas kernels: 37.9 us -> 34.4 us
    pallas_call x1, Pallas kernels: 37.2 us -> 33.6 us  [body(): pl.pallas_call(functools.partial(kernel, pb_size, ka_size), out_shape=(ja...]
where the time goes in v2:
time: 35.2 us; the launch traced here: 35 us
  Pallas kernels  34.4 us (98%)
  between operations  0.64 us (2%)
    pallas_call x1, Pallas kernels, body(): pl.pallas_call(functools.partial(kernel, pb_size, ka_size), out_shape=(ja...  33.6 us
    pallas_call x1, Pallas kernels, body(): pl.pallas_call(write_out, out_shape=tuple((jax.ShapeDtypeStruct(g.shape,...  0.74 us

profile of v2, /device:TPU:0, one launch (start us, length us, event | category | flops | bytes accessed | tf_op | source)
XLA Modules:
  0.0 35.0 jit_solution(1346518497406489640)
XLA Ops:
  0.6 33.6 %shard_map.103 = (bf16[128,1024]{1,0:T(8,128)(2,1)S(1)}, bf16[128,128]{1,0:T(8,128)(2,1)S(1)}, bf16[128,128]{1,0:T(8,128)(2,1)S(1)}) custom-call(bf16[128,1024]{1,0:T(8,128)(2,1)} %q_hbm.1, bf16[128,1024]{1,0:T(8,128)(2,1)} %g_hbm.1, bf16[128,1024]{1,0:T(8,128)(2,1)} %o_hbm.1, bf16[128,128]{1,0:T(8,128)(2,1)} %k_hbm.1, bf16[128,128]{1,0:T(8,128)(2,1)} %v_hbm.1, ...), custom_call_target="tpu_custom_call" | custom-call | tf_op jit(solution)/shard_map/pallas_call | solution.py:333
  34.3 0.7 %shard_map.104 = (bf16[128,1024]{1,0:T(8,128)(2,1)}, bf16[128,128]{1,0:T(8,128)(2,1)}, bf16[128,128]{1,0:T(8,128)(2,1)}) custom-call(bf16[128,1024]{1,0:T(8,128)(2,1)S(1)} %get-tuple-element.6.refs_0_, bf16[128,128]{1,0:T(8,128)(2,1)S(1)} %get-tuple-element.7.refs_1_, bf16[128,128]{1,0:T(8,128)(2,1)S(1)} %get-tuple-element.8.refs_2_), custom_call_target="tpu_custom_call" | custom-call | tf_op jit(solution)/shard_map/pallas_call | solution.py:372

commit v3 on v2

--- a/solution.py
+++ b/solution.py
@@ -121,8 +121,8 @@
         far = dz if dp == 3 and dz in direct else 0
         return remote(part.at[dz, dp], red.at[dz, dp], red_send.at[dz, dp], red_recv.at[dz, dp], place(far, dp))
 
-    def fold_copy(dz, dp):
-        return remote(part.at[dz, dp], fold.at[dz, dp], fold_send.at[dz, dp], fold_recv.at[dz, dp], place(dz, 0))
+    def fold_copy(dz):
+        return remote(part.at[dz, 3], fold.at[dz], fold_send.at[dz], fold_recv.at[dz], place(dz, 0))
 
     def z_copy(dz):
         return remote(zpart.at[dz], zred.at[dz], z_send.at[dz], z_recv.at[dz], place(dz, 0))
@@ -211,7 +211,7 @@
 
     def plane_sum(dz):
         total = acc[dz, 0]
-        for dp in () if dz in folded else (1, 2) if dz == 0 or dz in direct else (1, 2, 3):
+        for dp in (1, 2) if dz == 0 or dz in folded or dz in direct else (1, 2, 3):
             part_copy(dz, dp).wait_recv()
             total = total + red[dz, dp].astype(F32)
         return total
@@ -220,13 +220,13 @@
         zpart[dz] = plane_sum(dz).astype(BF16)
         z_copy(dz).start()
 
-    def merge(dp):
-        total = acc[0, dp]
+    def corner():
+        total = acc[0, 3]
         for dz in folded:
-            fold_copy(dz, dp).wait_recv()
-            total = total + fold[dz, dp].astype(F32)
-        part[0, dp] = total.astype(BF16)
-        part_copy(0, dp).start()
+            fold_copy(dz).wait_recv()
+            total = total + fold[dz].astype(F32)
+        part[0, 3] = total.astype(BF16)
+        part_copy(0, 3).start()
 
     def before(t):
         if t == when[0, 3]:
@@ -250,17 +250,16 @@
                     relay_copy(b[0], dp).wait_recv()
 
     def after(t):
-        for dz, dp in steps[t]:
-            if dp and dz in folded:
-                fold_copy(dz, dp).start()
-            elif dp and dz:
-                part_copy(dz, dp).start()
+        for b in reversed([b for s in steps for b in s]):
+            if b[1] and b != (0, 3) and min(last, when[b] + {0: 3}.get(b[0], 0)) == t:
+                if b[1] == 3 and b[0] in folded:
+                    fold_copy(b[0]).start()
+                else:
+                    part_copy(*b).start()
         if t == last:
-            for dp in (3, 1, 2):
-                merge(dp)
-        for dz in ranks[1:]:
-            ready = when[dz, 0] if dz in folded else max(when[dz, dp] for dp in range(3 if dz in direct else 4)) + 2
-            if min(ready, last) == t:
+            corner()
+        for dz in range(1, nz):
+            if max(when[dz, dp] for dp in range(3 if dz in direct else 4)) + 2 == t:
                 send_sum(dz)
 
     def pick(t, table):
@@ -279,6 +278,9 @@
 
     lax.fori_loop(0, len(steps), turn, 0)
     pair[3].start()
+    for dz in range(1, nz):
+        if max(when[dz, dp] for dp in range(3 if dz in direct else 4)) + 2 > last:
+            send_sum(dz)
     pair[3].wait_recv()
     for h in range(heads):
         dq = (dqt[0, h] + dqr[h]) * scale
@@ -298,15 +300,15 @@
     for copy in pair:
         copy.wait_send()
     for dz in range(nz):
-        for dp in (1, 2, 3):
-            if dz in folded:
-                fold_copy(dz, dp).wait_send()
-            else:
-                part_copy(dz, dp).wait_send()
         for dp in (1, 2):
+            part_copy(dz, dp).wait_send()
             plane_copy(dz, dp).wait_send()
             if dz > 0 and dz not in climb:
                 relay_copy(dz, dp).wait_send()
+        if dz in folded:
+            fold_copy(dz).wait_send()
+        else:
+            part_copy(dz, 3).wait_send()
         if dz > 0:
             column_copy(dz).wait_send()
             z_copy(dz).wait_send()
@@ -356,11 +358,11 @@
                 vmem((nz, plane, both, width), F32),
                 vmem((nz, both, width), BF16),
                 vmem((nz, both, width), BF16),
-                vmem((nz, plane, both, width), BF16),
+                vmem((nz, both, width), BF16),
                 dma((3 * heads + 2,)), dma((nz, plane)), dma((nz, plane)),
                 dma((nz, 2)), dma((nz, 2)), dma((4,)), dma((4,)),
                 dma((nz, plane)), dma((nz, plane)),
-                dma((nz,)), dma((nz,)), dma((nz, plane)), dma((nz, plane)),
+                dma((nz,)), dma((nz,)), dma((nz,)), dma((nz,)),
             ],
             compiler_params=pltpu.CompilerParams(
                 collective_id=0, has_side_effects=True, vmem_limit_bytes=48 * 2**20

time: 35.2 us -> 35.3 us (level)
  no operation moved by 1% of the time
where the time goes in v3:
time: 35.3 us; the launch traced here: 35.1 us
  Pallas kernels  34.5 us (98%)
  between operations  0.64 us (2%)
    pallas_call x1, Pallas kernels, body(): pl.pallas_call(functools.partial(kernel, pb_size, ka_size), out_shape=(ja...  33.7 us
    pallas_call x1, Pallas kernels, body(): pl.pallas_call(write_out, out_shape=tuple((jax.ShapeDtypeStruct(g.shape,...  0.74 us

profile of v3, /device:TPU:0, one launch (start us, length us, event | category | flops | bytes accessed | tf_op | source)
XLA Modules:
  0.0 35.1 jit_solution(10129880296686071573)
XLA Ops:
  0.6 33.7 %shard_map.103 = (bf16[128,1024]{1,0:T(8,128)(2,1)S(1)}, bf16[128,128]{1,0:T(8,128)(2,1)S(1)}, bf16[128,128]{1,0:T(8,128)(2,1)S(1)}) custom-call(bf16[128,1024]{1,0:T(8,128)(2,1)} %q_hbm.1, bf16[128,1024]{1,0:T(8,128)(2,1)} %g_hbm.1, bf16[128,1024]{1,0:T(8,128)(2,1)} %o_hbm.1, bf16[128,128]{1,0:T(8,128)(2,1)} %k_hbm.1, bf16[128,128]{1,0:T(8,128)(2,1)} %v_hbm.1, ...), custom_call_target="tpu_custom_call" | custom-call | tf_op jit(solution)/shard_map/pallas_call | solution.py:335
  34.4 0.7 %shard_map.104 = (bf16[128,1024]{1,0:T(8,128)(2,1)}, bf16[128,128]{1,0:T(8,128)(2,1)}, bf16[128,128]{1,0:T(8,128)(2,1)}) custom-call(bf16[128,1024]{1,0:T(8,128)(2,1)S(1)} %get-tuple-element.6.refs_0_, bf16[128,128]{1,0:T(8,128)(2,1)S(1)} %get-tuple-element.7.refs_1_, bf16[128,128]{1,0:T(8,128)(2,1)S(1)} %get-tuple-element.8.refs_2_), custom_call_target="tpu_custom_call" | custom-call | tf_op jit(solution)/shard_map/pallas_call | solution.py:374
